TPU v7x, 32 devices: a whole 2x2x4 slice. The times are simulated.
32 devices in a mesh: clip: 4 (over y, x), head: 8 (over z, core).
Axes of the slice: x: 2, y: 2, z: 4, core: 2. Of those that a mesh axis runs over, the one named last changes fastest.
Arguments:
- queries: bfloat16 [8192, 4096], P(('clip', 'head')), may hold values from -6 to 6
- key_rows: bfloat16 [8192, 4096], P(('clip', 'head')), may hold values from -6 to 6
- value_rows: bfloat16 [8192, 4096], P(('clip', 'head')), may hold values from -6 to 6
- query_tangent: bfloat16 [8192, 4096], P(('clip', 'head')), may hold values from -6 to 6
- key_tangent: bfloat16 [8192, 4096], P(('clip', 'head')), may hold values from -6 to 6
- value_tangent: bfloat16 [8192, 4096], P(('clip', 'head')), may hold values from -6 to 6
- partners: int32 [8, 2], replicated, may hold values from 0 to 7, as said below
- cotangent: bfloat16 [8192, 3072], P('clip'), may hold values from -6 to 6
Outputs:
- attended: bfloat16 [8192, 4096], P(('clip', 'head'))
- attended_tangent: bfloat16 [8192, 4096], P(('clip', 'head'))
- weight_grad: float32 [3072, 4096], P('clip', 'head')
Inputs may be any that keep to these rules, and one draw needn't show every extreme that they name: `partners`: for clip c the two entries are distinct clips (c - d) mod 8 with 1 <= d <= 2 + c % 2.
All inputs are finite; a program needn't handle non-finite values.
Results may differ from a plain program's by a relative error of at most 0.0051.
Values may be sent and summed in bfloat16 or wider, within the bound.
A program may use at most 192 MiB of HBM per device.

v0:
```python
import functools
import math

import jax
import jax.numpy as jnp
from jax import lax
from jax.experimental import pallas as pl
from jax.experimental.pallas import tpu as pltpu
from jax.sharding import PartitionSpec as P

HDIM = 128
CLIP = 1024
NT = (((1,), (1,)), ((), ()))
MESH = pl.DeviceIdType.MESH


def attend_rows(both, wk, wv, scale):
    f32 = jnp.float32
    scores = lax.dot_general(both[:, HDIM:], wk[:, :HDIM], NT, preferred_element_type=f32)
    score_tan = lax.dot_general(both, wk[...], NT, preferred_element_type=f32)
    row_max = jnp.max(scores, axis=1, keepdims=True)
    weights = jnp.exp2((scores - row_max) * (scale * math.log2(math.e)))
    inverse = 1.0 / jnp.sum(weights, axis=1, keepdims=True)
    mean = jnp.sum(weights * score_tan, axis=1, keepdims=True) * inverse
    low = weights.astype(jnp.bfloat16)
    tan_low = (weights * (score_tan - mean)).astype(jnp.bfloat16)
    first = jnp.dot(low, wv[...], preferred_element_type=f32)
    second = jnp.dot(tan_low, wv[:, :HDIM], preferred_element_type=f32)
    out = first[:, :HDIM] * inverse
    tan = (first[:, HDIM:] + second * scale) * inverse
    return out.astype(jnp.bfloat16), tan.astype(jnp.bfloat16)


KV, QS = (0, 1, 2, 3), (4, 5)


def exchange_kernel(n, clips, heads, flags, *refs):
    args, (out, tan) = refs[:6], refs[6:8]
    kk, vv, qq = refs[8 : 8 + heads], refs[8 + heads : 8 + 2 * heads], refs[8 + 2 * heads : 8 + 3 * heads]
    wk, wv, send, recv, local, fsend, frecv = refs[8 + 3 * heads :]
    piece = args[0].shape[0]
    rows = n * piece
    me, group = lax.axis_index("head"), lax.axis_index("clip")
    after, before = lax.rem(group + 1, clips), lax.rem(group + clips - 1, clips)
    if n & (n - 1) == 0:
        steps = [d for bit in range(n.bit_length() - 2, -1, -1) for d in range(1 << bit, 2 << bit)]
        peers = [(me ^ d, me ^ d) for d in steps]
    else:
        peers = [(lax.rem(me + d, n), lax.rem(me + n - d, n)) for d in range(1, n)]

    barrier = pltpu.get_barrier_semaphore()
    for to, _ in peers:
        pl.semaphore_signal(barrier, inc=1, device_id={"head": to}, device_id_type=MESH)
    for to in (after, before):
        pl.semaphore_signal(barrier, inc=1, device_id={"clip": to}, device_id_type=MESH)
    pl.semaphore_wait(barrier, n + 1)

    def landing(head, t, source):
        buffer, base = ((kk, rows), (vv, rows), (qq, 0))[t // 2]
        at = pl.ds(pl.multiple_of(base + source * piece, piece), piece)
        return buffer[head].at[at, pl.ds(HDIM * (t % 2), HDIM)]

    def column(head, t, owner):
        at = pl.ds(pl.multiple_of((owner * heads + head) * HDIM, HDIM), HDIM)
        return args[t].at[:, at]

    def outgoing(head, t, to):
        return pltpu.make_async_remote_copy(
            src_ref=column(head, t, to),
            dst_ref=landing(head, t, me),
            send_sem=send.at[head, t, to],
            recv_sem=recv.at[head, t, me],
            device_id={"head": to},
            device_id_type=MESH,
        )

    def incoming(head, t, source):
        return pltpu.make_async_remote_copy(
            src_ref=column(head, t, source),
            dst_ref=landing(head, t, source),
            send_sem=send.at[head, t, source],
            recv_sem=recv.at[head, t, source],
            device_id={"head": source},
            device_id_type=MESH,
        )

    def stay(head, t):
        return pltpu.make_async_copy(column(head, t, me), landing(head, t, me), local.at[head, t])

    def forward(head, which):
        buffer = (kk, vv)[which][head]
        return pltpu.make_async_remote_copy(
            src_ref=buffer.at[pl.ds(rows, rows)],
            dst_ref=buffer.at[pl.ds(0, rows)],
            send_sem=fsend.at[head, which],
            recv_sem=frecv.at[head, which],
            device_id={"clip": after},
            device_id_type=MESH,
        )

    def issue(stage):
        head, tensors = stage
        for t in tensors:
            for to, _ in peers:
                outgoing(head, t, to).start()
            stay(head, t).start()

    def arrive(stage):
        head, tensors = stage
        for t in tensors:
            stay(head, t).wait()
            for _, source in peers:
                incoming(head, t, source).wait_recv()

    clip_count = rows // CLIP
    block_rows = min(256, CLIP)

    def attend(head):
        def one_clip(within, _):
            own = clip_count + within
            for place in range(3):
                at = pl.ds(place * CLIP, CLIP)
                for window, held in ((wk, kk[head]), (wv, vv[head])):

                    def clip_back(gap):
                        row = pl.multiple_of(lax.max(own - gap, 0) * CLIP, CLIP)
                        return held[pl.ds(row, CLIP), :].reshape(CLIP // 16, 16, 2 * HDIM)

                    if place == 0:
                        window[at, :] = held[pl.ds(pl.multiple_of(own * CLIP, CLIP), CLIP), :]
                    else:
                        flag = (within * 2 + place - 1) * 2
                        mixed = clip_back(place) * flags[flag] + clip_back(place + 1) * flags[flag + 1]
                        window[at, :] = mixed.reshape(CLIP, 2 * HDIM)

            def one_block(block, _):
                at = pl.ds(pl.multiple_of(within * CLIP + block * block_rows, block_rows), block_rows)
                cols = pl.ds(head * HDIM, HDIM)
                out[at, cols], tan[at, cols] = attend_rows(qq[head][at, :], wk, wv, HDIM**-0.5)
                return 0

            return lax.fori_loop(0, CLIP // block_rows, one_block, 0)

        lax.fori_loop(0, clip_count, one_clip, 0)

    stages = []
    for head in range(heads):
        stages.append((head, KV))
        if head:
            stages.append((head - 1, QS))
    stages.append((heads - 1, QS))
    ahead = 2
    for stage in stages[:ahead]:
        issue(stage)
    for number, stage in enumerate(stages):
        arrive(stage)
        if number + ahead < len(stages):
            issue(stages[number + ahead])
        head, tensors = stage
        if tensors is KV:
            for which in range(2):
                forward(head, which).start()
        else:
            for which in range(2):
                forward(head, which).wait_recv()
            attend(head)
    for head in range(heads):
        for which in range(2):
            forward(head, which).wait_send()
        for t in range(6):
            for to, _ in peers:
                outgoing(head, t, to).wait_send()


def exchange_and_attend(flags, args):
    n, clips = lax.axis_size("head"), lax.axis_size("clip")
    rows, cols = args[0].shape[0] * n, args[0].shape[1] // n
    heads = cols // HDIM
    low = jnp.bfloat16
    shape = jax.ShapeDtypeStruct((rows, cols), low)
    dma = pltpu.SemaphoreType.DMA
    return pl.pallas_call(
        functools.partial(exchange_kernel, n, clips, heads),
        out_shape=(shape, shape),
        in_specs=[pl.BlockSpec(memory_space=pltpu.VMEM)] + [pl.BlockSpec(memory_space=pl.ANY)] * 6,
        out_specs=[pl.BlockSpec(memory_space=pltpu.VMEM)] * 2,
        scratch_shapes=[pltpu.VMEM((2 * rows, 2 * HDIM), low)] * (2 * heads)
        + [pltpu.VMEM((rows, 2 * HDIM), low)] * heads
        + [pltpu.VMEM((3 * CLIP, 2 * HDIM), low)] * 2
        + [dma((heads, 6, n)), dma((heads, 6, n)), dma((heads, 6)), dma((heads, 2)), dma((heads, 2))],
        compiler_params=pltpu.CompilerParams(
            collective_id=0, has_side_effects=True, vmem_limit_bytes=60 * 1024 * 1024
        ),
        cost_estimate=pl.CostEstimate(
            flops=12 * rows * cols * 3 * CLIP,
            bytes_accessed=12 * rows * cols * 2,
            transcendentals=rows * heads * 3 * CLIP,
        ),
    )(flags, *args)


def on_device(
    queries, key_rows, value_rows, query_tangent, key_tangent, value_tangent, partners, cotangent
):
    clip_count, head_count = lax.axis_size("clip"), lax.axis_size("head")
    clips_here = queries.shape[0] * head_count // CLIP
    first_clip = lax.axis_index("clip") * clips_here
    mine = lax.dynamic_slice_in_dim(partners, first_clip, clips_here, 0)
    clip_ids = first_clip + jnp.arange(clips_here, dtype=jnp.int32)
    gaps = (clip_ids[:, None] - mine) % (clips_here * clip_count)
    near, far = jnp.min(gaps, axis=1) == 1, jnp.max(gaps, axis=1) == 2
    flags = jnp.stack([near, ~near, far, ~far], axis=1).reshape(-1, 1, 1).astype(jnp.bfloat16)
    flags = jnp.broadcast_to(flags, (4 * clips_here, 16, 2 * HDIM))
    args = (key_rows, key_tangent, value_rows, value_tangent, query_tangent, queries)
    output_h, tangent_h = exchange_and_attend(flags, args)
    partial_term = lax.dot_general(
        cotangent, output_h, (((0,), (0,)), ((), ())), preferred_element_type=jnp.float32
    )
    weight_grad = lax.psum_scatter(partial_term, "clip", scatter_dimension=0, tiled=True)

    def to_tokens(a):
        return lax.all_to_all(a, "head", split_axis=0, concat_axis=1, tiled=True)

    return (to_tokens(output_h), to_tokens(tangent_h), weight_grad)


def solution(mesh):
    tokens = P(("clip", "head"), None)
    return jax.shard_map(
        on_device,
        mesh=mesh,
        in_specs=(tokens,) * 6 + (P(), P("clip", None)),
        out_specs=(tokens, tokens, P("clip", "head")),
        check_vma=False,
    )
```

profile of v0, /device:TPU:9, one launch (start us, length us, event | category | flops | bytes accessed | tf_op | source)
XLA Modules:
  0.0 452.4 jit_solution(4405801028491332299)
XLA Ops:
  7.2 0.0 reduce-scatter.2.cloned.1.call-start
  7.2 0.8 fusion.1
  8.0 0.1 copy.17
  8.1 0.1 copy.18
  8.3 0.1 add_convert_fusion
  8.3 0.1 reshape.58
  8.4 0.7 broadcast_in_dim.2.flags
  9.1 315.7 %shard_map.103 = (bf16[2048,512]{1,0:T(8,128)(2,1)}, bf16[2048,512]{1,0:T(8,128)(2,1)}) custom-call(bf16[8,16,256]{2,1,0:T(8,128)(2,1)} %broadcast_in_dim.2.flags, bf16[256,4096]{1,0:T(8,128)(2,1)} %refs_0_.1, bf16[256,4096]{1,0:T(8,128)(2,1)} %refs_1_.1, bf16[256,4096]{1,0:T(8,128)(2,1)} %refs_2_.1, bf16[256,4096]{1,0:T(8,128)(2,1)} %refs_3_.1, ...), custom_call_target="tpu_custom_call" | custom-call | flops 38654705664 | bytes 25165824 | tf_op jit(solution)/shard_map/pallas_call | solution.py:182
  324.8 12.1 %convolution_bitcast_fusion = f32[3072,512]{0,1:T(8,128)} fusion(bf16[2048,512]{1,0:T(8,128)(2,1)} %get-tuple-element.5, bf16[2048,3072]{1,0:T(8,128)(2,1)} %param.15), kind=kOutput, calls=%fused_computation | convolution fusion | flops 6442450944 | bytes 20971520 | tf_op jit(solution)/shard_map/dot_general | solution.py:216
  336.9 0.0 copy-start
  336.9 0.0 reduce-scatter.2.cloned.1.call-update
  336.9 1.6 copy-done
  338.5 50.4 %all_to_all.38 = bf16[8,256,512]{2,1,0:T(8,128)(2,1)} all-to-all(bf16[8,256,512]{2,1,0:T(8,128)(2,1)S(1)} %bitcast.21), channel_id=1, replica_groups=mesh['clip'=4,'head'=8] {'head'}, dimensions={0} | all-to-all | bytes 4194304 | tf_op jit(solution)/shard_map/all_to_all | solution.py:222
  388.9 6.5 %all-to-all-start = ((bf16[8,256,512]{2,1,0:T(8,128)(2,1)}), bf16[8,256,512]{2,1,0:T(8,128)(2,1)S(1)}, u32[]{:S(2)}, u32[]{:S(2)}) async-start(bf16[8,256,512]{2,1,0:T(8,128)(2,1)} %bitcast.19), calls=%async_computation | async-start | bytes 4194304 | tf_op jit(solution)/shard_map/all_to_all | solution.py:222
  395.4 3.3 copy.23
  398.7 42.3 %all-to-all-done = bf16[8,256,512]{2,1,0:T(8,128)(2,1)S(1)} async-done(((bf16[8,256,512]{2,1,0:T(8,128)(2,1)}), bf16[8,256,512]{2,1,0:T(8,128)(2,1)S(1)}, u32[]{:S(2)}, u32[]{:S(2)}) %all-to-all-start) | async-done | bytes 2097184 | tf_op jit(solution)/shard_map/all_to_all | solution.py:222
  440.9 1.6 copy.22
  442.5 0.0 reduce-scatter.2.cloned.1.call-done
  442.5 3.0 copy.21
  (4 shorter events, 0.0 us)
Async XLA Ops:
  7.2 435.4 %reduce-scatter.2.cloned.1.call-start = ((), (), s32[]{:S(2)}) async-start(), calls=%async_computation.3 | async-start | bytes 7864320 | tf_op jit(solution)/shard_map/reduce_scatter | solution.py:219
  336.9 1.6 copy-start
  388.9 52.0 %all-to-all-start = ((bf16[8,256,512]{2,1,0:T(8,128)(2,1)}), bf16[8,256,512]{2,1,0:T(8,128)(2,1)S(1)}, u32[]{:S(2)}, u32[]{:S(2)}) async-start(bf16[8,256,512]{2,1,0:T(8,128)(2,1)} %bitcast.19), calls=%async_computation | async-start | bytes 4194304 | tf_op jit(solution)/shard_map/all_to_all | solution.py:222
Sparse Core Ops, SparseCore 0:
  337.0 68.0 reduce-scatter.1
where the time goes:
time: 457 us; the launch traced here: 452 us
  Pallas kernels  316 us (69%)
  blocking collectives  50.4 us (11%)
  waiting for transfers between devices  42.3 us (9%)
  between operations  14.1 us (3%)
  matrix products  12.1 us (3%)
  local copies, waits for them, and re-layouts  10.5 us (2%)
  starting transfers between devices  6.55 us (1%)
    pallas_call x1, Pallas kernels, exchange_and_attend(): pl.pallas_call(functools.partial(exchange_kernel, n, clips, heads), out_s...  316 us
    all_to_all x1, blocking collectives, to_tokens(): return lax.all_to_all(a, 'head', split_axis=0, concat_axis=1, tiled=True)  50.4 us
    all_to_all x1, waiting for transfers between devices, to_tokens(): return lax.all_to_all(a, 'head', split_axis=0, concat_axis=1, tiled=True)  42.3 us
    dot_general x1, matrix products, on_device(): lax.dot_general(cotangent, output_h, (((0,), (0,)), ((), ())), preferred_...  12.1 us
  transfers between devices with their start and end apart: 2, of which 1 were waited for; matrix products, arithmetic and copies ran while one was open for 1% of the time, Pallas kernels for 0%

commit v1 on v0

v1 whole, which is shorter than its diff:
```python
import functools
import math

import jax
import jax.numpy as jnp
from jax import lax
from jax.experimental import pallas as pl
from jax.experimental.pallas import tpu as pltpu
from jax.sharding import PartitionSpec as P

HDIM = 128
CLIP = 1024
AHEAD = 4
NT = (((1,), (1,)), ((), ()))
MESH = pl.DeviceIdType.MESH


def attend_rows(both, wk, wv, scale):
    f32 = jnp.float32
    scores = lax.dot_general(both[:, HDIM:], wk[:, :HDIM], NT, preferred_element_type=f32)
    score_tan = lax.dot_general(both, wk[...], NT, preferred_element_type=f32)
    row_max = jnp.max(scores, axis=1, keepdims=True)
    weights = jnp.exp2((scores - row_max) * (scale * math.log2(math.e)))
    inverse = 1.0 / jnp.sum(weights, axis=1, keepdims=True)
    mean = jnp.sum(weights * score_tan, axis=1, keepdims=True) * inverse
    low = weights.astype(jnp.bfloat16)
    tan_low = (weights * (score_tan - mean)).astype(jnp.bfloat16)
    first = jnp.dot(low, wv[...], preferred_element_type=f32)
    second = jnp.dot(tan_low, wv[:, :HDIM], preferred_element_type=f32)
    out = first[:, :HDIM] * inverse
    tan = (first[:, HDIM:] + second * scale) * inverse
    return out.astype(jnp.bfloat16), tan.astype(jnp.bfloat16)


KEYS, VALUES, QUERIES = (0, 1), (2, 3), (4, 5)


def exchange_kernel(n, clips, heads, partners, *refs):
    args, cotangent, (out, tan, grad) = refs[:6], refs[6], refs[7:10]
    refs = refs[10:]
    kk, vv, qq, oo = (refs[i * heads : (i + 1) * heads] for i in range(4))
    wk, wv, cot, flipped, terms, others = refs[4 * heads : 4 * heads + 6]
    send, recv, local, fsend, frecv, osend, orecv, olocal, gsend, grecv, csem = refs[4 * heads + 6 :]
    piece = args[0].shape[0]
    rows = n * piece
    wide = cot.shape[1] // clips
    me, group = lax.axis_index("head"), lax.axis_index("clip")
    after, before = lax.rem(group + 1, clips), lax.rem(group + clips - 1, clips)
    if n & (n - 1) == 0:
        steps = [d for bit in range(n.bit_length() - 2, -1, -1) for d in range(1 << bit, 2 << bit)]
        peers = [(me ^ d, me ^ d) for d in steps]
    else:
        peers = [(lax.rem(me + d, n), lax.rem(me + n - d, n)) for d in range(1, n)]
    groups = [(lax.rem(group + d, clips), lax.rem(group + clips - d, clips)) for d in range(1, clips)]

    barrier = pltpu.get_barrier_semaphore()
    for to, _ in peers:
        pl.semaphore_signal(barrier, inc=1, device_id={"head": to}, device_id_type=MESH)
    for to, _ in groups:
        pl.semaphore_signal(barrier, inc=1, device_id={"clip": to}, device_id_type=MESH)
    pl.semaphore_wait(barrier, n - 1 + clips - 1)

    def landing(head, t, source):
        buffer, base = ((kk, rows), (vv, rows), (qq, 0))[t // 2]
        at = pl.ds(pl.multiple_of(base + source * piece, piece), piece)
        return buffer[head].at[at, pl.ds(HDIM * (t % 2), HDIM)]

    def column(head, t, owner):
        at = pl.ds(pl.multiple_of((owner * heads + head) * HDIM, HDIM), HDIM)
        return args[t].at[:, at]

    def outgoing(head, t, to):
        return pltpu.make_async_remote_copy(
            src_ref=column(head, t, to),
            dst_ref=landing(head, t, me),
            send_sem=send.at[head, t, to],
            recv_sem=recv.at[head, t, me],
            device_id={"head": to},
            device_id_type=MESH,
        )

    def incoming(head, t, source):
        return pltpu.make_async_remote_copy(
            src_ref=column(head, t, source),
            dst_ref=landing(head, t, source),
            send_sem=send.at[head, t, source],
            recv_sem=recv.at[head, t, source],
            device_id={"head": source},
            device_id_type=MESH,
        )

    def stay(head, t):
        return pltpu.make_async_copy(column(head, t, me), landing(head, t, me), local.at[head, t])

    def forward(head, which):
        buffer = (kk, vv)[which][head]
        return pltpu.make_async_remote_copy(
            src_ref=buffer.at[pl.ds(rows, rows)],
            dst_ref=buffer.at[pl.ds(0, rows)],
            send_sem=fsend.at[head, which],
            recv_sem=frecv.at[head, which],
            device_id={"clip": after},
            device_id_type=MESH,
        )

    def issue(stage):
        head, tensors = stage
        for t in tensors:
            for to, _ in peers:
                outgoing(head, t, to).start()
            stay(head, t).start()

    def arrive(stage):
        head, tensors = stage
        for t in tensors:
            stay(head, t).wait()
            for _, source in peers:
                incoming(head, t, source).wait_recv()

    def result_rows(head, which, owner):
        at = pl.ds(pl.multiple_of(owner * piece, piece), piece)
        return oo[head].at[at, pl.ds(HDIM * which, HDIM)]

    def result_home(head, which, maker):
        at = pl.ds(pl.multiple_of((maker * heads + head) * HDIM, HDIM), HDIM)
        return (out, tan)[which].at[:, at]

    def give(head, which, to):
        return pltpu.make_async_remote_copy(
            src_ref=result_rows(head, which, to),
            dst_ref=result_home(head, which, me),
            send_sem=osend.at[head, which, to],
            recv_sem=orecv.at[head, which, me],
            device_id={"head": to},
            device_id_type=MESH,
        )

    def take(head, which, maker):
        return pltpu.make_async_remote_copy(
            src_ref=result_rows(head, which, maker),
            dst_ref=result_home(head, which, maker),
            send_sem=osend.at[head, which, maker],
            recv_sem=orecv.at[head, which, maker],
            device_id={"head": maker},
            device_id_type=MESH,
        )

    def keep(head, which):
        return pltpu.make_async_copy(
            result_rows(head, which, me), result_home(head, which, me), olocal.at[head, which]
        )

    def hand_out(head, owner):
        @pl.when(owner == me)
        def _():
            for which in range(2):
                keep(head, which).start()

        @pl.when(owner != me)
        def _():
            for which in range(2):
                give(head, which, owner).start()

    clip_count = rows // CLIP
    block_rows = min(256, piece)
    per_clip, per_piece = CLIP // block_rows, piece // block_rows
    total_clips = clip_count * clips
    home = me * piece // CLIP

    def block_of(step):
        within = lax.rem(home + 1 + step // per_clip, clip_count)
        return within * per_clip + lax.rem(step, per_clip)

    def is_one(value):
        return jnp.full((16, 2 * HDIM), jnp.where(value, 1.0, 0.0), jnp.float32).astype(jnp.bfloat16)

    def attend(head):
        def one_clip(turn, _):
            within = lax.rem(home + 1 + turn, clip_count)
            own = clip_count + within
            clip_id = group * clip_count + within
            gaps = [lax.rem(clip_id - partners[clip_id, i] + total_clips, total_clips) for i in range(2)]
            near, far = jnp.minimum(*gaps) == 1, jnp.maximum(*gaps) == 2
            flags = [is_one(near), is_one(jnp.logical_not(near)), is_one(far), is_one(jnp.logical_not(far))]
            for place in range(3):
                at = pl.ds(place * CLIP, CLIP)
                for window, held in ((wk, kk[head]), (wv, vv[head])):

                    def clip_back(gap):
                        row = pl.multiple_of(lax.max(own - gap, 0) * CLIP, CLIP)
                        return held[pl.ds(row, CLIP), :].reshape(CLIP // 16, 16, 2 * HDIM)

                    if place == 0:
                        window[at, :] = held[pl.ds(pl.multiple_of(own * CLIP, CLIP), CLIP), :]
                    else:
                        flag = (place - 1) * 2
                        mixed = clip_back(place) * flags[flag] + clip_back(place + 1) * flags[flag + 1]
                        window[at, :] = mixed.reshape(CLIP, 2 * HDIM)

            def one_block(block, _):
                row = within * CLIP + block * block_rows
                at = pl.ds(pl.multiple_of(row, block_rows), block_rows)
                step = turn * per_clip + block
                result = attend_rows(qq[head][at, :], wk, wv, HDIM**-0.5)
                oo[head][at, :HDIM], oo[head][at, HDIM:] = result

                @pl.when(jnp.logical_and(step > 0, lax.rem(step, per_piece) == 0))
                def _():
                    hand_out(head, block_of(step - 1) // per_piece)

                return 0

            return lax.fori_loop(0, per_clip, one_block, 0)

        lax.fori_loop(0, clip_count, one_clip, 0)

    tile = 256 if cot.shape[1] % 256 == 0 else HDIM

    def multiply(head):
        flipped[...] = oo[head][:, :HDIM].T

        def one_tile(j, _):
            at = pl.ds(pl.multiple_of(j * tile, tile), tile)
            terms[head % 2, :, at] = jnp.dot(
                flipped[...], cot[:, at], preferred_element_type=jnp.float32
            )
            return 0

        lax.fori_loop(0, cot.shape[1] // tile, one_tile, 0)

    def share(owner):
        return pl.ds(pl.multiple_of(owner * wide, HDIM), wide)

    def give_term(head, to, source):
        return pltpu.make_async_remote_copy(
            src_ref=terms.at[head % 2, :, share(to)],
            dst_ref=others.at[head, source],
            send_sem=gsend.at[head, to],
            recv_sem=grecv.at[head, source],
            device_id={"clip": to},
            device_id_type=MESH,
        )

    def reduce_terms(head):
        total = terms[head % 2, :, share(group)]
        for _, source in groups:
            give_term(head, source, source).wait_recv()
            total = total + others[head, source]
        grad[:, head * HDIM : (head + 1) * HDIM] = total.T

    stages = []
    for head in range(heads):
        stages += [(head, KEYS), (head, VALUES)]
        if head:
            stages.append((head - 1, QUERIES))
    stages.append((heads - 1, QUERIES))
    load = pltpu.make_async_copy(cotangent, cot, csem)
    for stage in stages[:AHEAD]:
        issue(stage)
    load.start()
    for number, stage in enumerate(stages):
        arrive(stage)
        if number + AHEAD < len(stages):
            issue(stages[number + AHEAD])
        head, tensors = stage
        if tensors is not QUERIES:
            forward(head, tensors[0] // 2).start()
            continue
        for which in range(2):
            forward(head, which).wait_recv()
        attend(head)
        if head == 0:
            load.wait()
        if head >= 2:
            for to, _ in groups:
                give_term(head - 2, to, group).wait_send()
        multiply(head)
        hand_out(head, block_of(rows // block_rows - 1) // per_piece)
        for to, _ in groups:
            give_term(head, to, group).start()
        if head:
            reduce_terms(head - 1)
    reduce_terms(heads - 1)
    for head in range(heads):
        for which in range(2):
            forward(head, which).wait_send()
            keep(head, which).wait()
            for to, maker in peers:
                give(head, which, to).wait_send()
                take(head, which, maker).wait_recv()
        for t in range(6):
            for to, _ in peers:
                outgoing(head, t, to).wait_send()
    for head in range(max(heads - 2, 0), heads):
        for to, _ in groups:
            give_term(head, to, group).wait_send()


def on_device(
    queries, key_rows, value_rows, query_tangent, key_tangent, value_tangent, partners, cotangent
):
    n, clips = lax.axis_size("head"), lax.axis_size("clip")
    rows, cols = queries.shape[0] * n, queries.shape[1] // n
    heads = cols // HDIM
    width = cotangent.shape[1]
    args = (key_rows, key_tangent, value_rows, value_tangent, query_tangent, queries)
    low, f32 = jnp.bfloat16, jnp.float32
    like = jax.ShapeDtypeStruct(queries.shape, low)
    dma = pltpu.SemaphoreType.DMA
    hbm = pl.BlockSpec(memory_space=pl.ANY)
    return pl.pallas_call(
        functools.partial(exchange_kernel, n, clips, heads),
        out_shape=(like, like, jax.ShapeDtypeStruct((width // clips, cols), f32)),
        in_specs=[pl.BlockSpec(memory_space=pltpu.SMEM)] + [hbm] * 7,
        out_specs=[hbm, hbm, pl.BlockSpec(memory_space=pltpu.VMEM)],
        scratch_shapes=[pltpu.VMEM((2 * rows, 2 * HDIM), low)] * (2 * heads)
        + [pltpu.VMEM((rows, 2 * HDIM), low)] * (2 * heads)
        + [pltpu.VMEM((3 * CLIP, 2 * HDIM), low)] * 2
        + [
            pltpu.VMEM((rows, width), low),
            pltpu.VMEM((HDIM, rows), low),
            pltpu.VMEM((2, HDIM, width), f32),
            pltpu.VMEM((heads, clips, HDIM, width // clips), f32),
        ]
        + [dma((heads, 6, n)), dma((heads, 6, n)), dma((heads, 6)), dma((heads, 2)), dma((heads, 2))]
        + [dma((heads, 2, n)), dma((heads, 2, n)), dma((heads, 2))]
        + [dma((heads, clips)), dma((heads, clips)), dma],
        compiler_params=pltpu.CompilerParams(
            collective_id=0, has_side_effects=True, vmem_limit_bytes=63 * 1024 * 1024
        ),
        cost_estimate=pl.CostEstimate(
            flops=12 * rows * cols * 3 * CLIP + 2 * rows * cols * width,
            bytes_accessed=16 * rows * cols * 2 + rows * width * 2,
            transcendentals=rows * heads * 3 * CLIP,
        ),
    )(partners, *args, cotangent)


def solution(mesh):
    tokens = P(("clip", "head"), None)
    return jax.shard_map(
        on_device,
        mesh=mesh,
        in_specs=(tokens,) * 6 + (P(), P("clip", None)),
        out_specs=(tokens, tokens, P("clip", "head")),
        check_vma=False,
    )
```

time: 457 us -> 382 us (0.84); the launches traced: 452 us -> 382 us
  Pallas kernels: 316 us -> 373 us
  blocking collectives: 50.4 us -> 0 us
  waiting for transfers between devices: 42.3 us -> 0 us
  between operations: 14.1 us -> 0.65 us
  matrix products: 12.1 us -> 0 us
  starting transfers between devices: 6.55 us -> 0 us
    pallas_call x1, Pallas kernels: 316 us -> 373 us  [on_device(): pl.pallas_call(functools.partial(exchange_kernel, n, clips, heads), out_s...]
    all_to_all x1 -> x0, blocking collectives: 50.4 us -> none  [to_tokens(): return lax.all_to_all(a, 'head', split_axis=0, concat_axis=1, tiled=True)]
    all_to_all x1 -> x0, waiting for transfers between devices: 42.3 us -> none  [to_tokens(): return lax.all_to_all(a, 'head', split_axis=0, concat_axis=1, tiled=True)]
    dot_general x1 -> x0, matrix products: 12.1 us -> none  [on_device(): lax.dot_general(cotangent, output_h, (((0,), (0,)), ((), ())), preferred_...]
    all_to_all x1 -> x0, starting transfers between devices: 6.52 us -> none  [to_tokens(): return lax.all_to_all(a, 'head', split_axis=0, concat_axis=1, tiled=True)]
    all_to_all x2 -> x0, local copies, waits for them, and re-layouts: 4.87 us -> none  [to_tokens(): return lax.all_to_all(a, 'head', split_axis=0, concat_axis=1, tiled=True)]
  transfers between devices with their start and end apart: 2 -> 0, of which waited for: 1 -> 0; matrix products, arithmetic and copies ran while one was open for 1% -> 0% of each run, Pallas kernels for 0% -> 0%
where the time goes in v1:
time: 382 us
  Pallas kernels  373 us (98%)
  local copies, waits for them, and re-layouts  7.93 us (2%)
    pallas_call x1, Pallas kernels, on_device(): pl.pallas_call(functools.partial(exchange_kernel, n, clips, heads), out_s...  373 us
    unnamed x8, local copies, waits for them, and re-layouts  7.93 us

profile of v1, /device:TPU:9, one launch (start us, length us, event | category | flops | bytes accessed | tf_op | source)
XLA Modules:
  0.0 382.1 jit_solution(15547007117746881306)
XLA Ops:
  0.6 1.3 copy.11.partners
  2.0 373.5 %shard_map.103 = (bf16[256,4096]{1,0:T(8,128)(2,1)}, bf16[256,4096]{1,0:T(8,128)(2,1)}, f32[768,512]{1,0:T(8,128)}) custom-call(s32[8,2]{1,0:T(8,128)} %copy.11.partners, bf16[256,4096]{1,0:T(8,128)(2,1)} %refs_0_.1, bf16[256,4096]{1,0:T(8,128)(2,1)} %refs_1_.1, bf16[256,4096]{1,0:T(8,128)(2,1)} %refs_2_.1, bf16[256,4096]{1,0:T(8,128)(2,1)} %refs_3_.1, ...), custom_call_target="tpu_custom_call" | custom-call | flops 45097156608 | bytes 46137344 | tf_op jit(solution)/shard_map/pallas_call | solution.py:311
  375.5 0.0 copy-start
  375.5 3.3 copy.15
  378.7 0.0 copy-done
  378.7 0.0 copy-start.1
  378.8 1.3 copy.16
  380.1 0.8 copy-done.1
  380.9 1.1 copy.17
Async XLA Ops:
  375.5 3.3 copy-start
  378.7 2.2 copy-start.1

commit v2 on v1

v2 whole, which is shorter than its diff:
```python
import functools
import math

import jax
import jax.numpy as jnp
from jax import lax
from jax.experimental import pallas as pl
from jax.experimental.pallas import tpu as pltpu
from jax.sharding import PartitionSpec as P

HDIM = 128
CLIP = 1024
AHEAD = 4
NT = (((1,), (1,)), ((), ()))
MESH = pl.DeviceIdType.MESH


def attend_rows(both, wk, wv, scale):
    f32 = jnp.float32
    scores = lax.dot_general(both[:, HDIM:], wk[:, :HDIM], NT, preferred_element_type=f32)
    score_tan = lax.dot_general(both, wk[...], NT, preferred_element_type=f32)
    row_max = jnp.max(scores, axis=1, keepdims=True)
    weights = jnp.exp2((scores - row_max) * (scale * math.log2(math.e)))
    inverse = 1.0 / jnp.sum(weights, axis=1, keepdims=True)
    mean = jnp.sum(weights * score_tan, axis=1, keepdims=True) * inverse
    low = weights.astype(jnp.bfloat16)
    tan_low = (weights * (score_tan - mean)).astype(jnp.bfloat16)
    first = jnp.dot(low, wv[...], preferred_element_type=f32)
    second = jnp.dot(tan_low, wv[:, :HDIM], preferred_element_type=f32)
    out = first[:, :HDIM] * inverse
    tan = (first[:, HDIM:] + second * scale) * inverse
    return out.astype(jnp.bfloat16), tan.astype(jnp.bfloat16)


def exchange_kernel(n, clips, heads, partners, *refs):
    args, cotangent, (out, tan, grad) = refs[:6], refs[6], refs[7:10]
    kk, vv, qq, oo, wk, wv, cot, flipped, terms, others, chosen = refs[10:21]
    send, recv, local, fsend, frecv, osend, orecv, olocal, gsend, grecv, csem = refs[21:]
    piece = args[0].shape[0]
    rows = n * piece
    wide = cot.shape[1] // clips
    me, group = lax.axis_index("head"), lax.axis_index("clip")
    after = lax.rem(group + 1, clips)
    if n & (n - 1) == 0:
        steps = [d for bit in range(n.bit_length() - 2, -1, -1) for d in range(1 << bit, 2 << bit)]
        peers = [(me ^ d, me ^ d) for d in steps]
    else:
        peers = [(lax.rem(me + d, n), lax.rem(me + n - d, n)) for d in range(1, n)]
    groups = [(lax.rem(group + d, clips), lax.rem(group + clips - d, clips)) for d in range(1, clips)]

    barrier = pltpu.get_barrier_semaphore()
    for to, _ in peers:
        pl.semaphore_signal(barrier, inc=1, device_id={"head": to}, device_id_type=MESH)
    for to, _ in groups:
        pl.semaphore_signal(barrier, inc=1, device_id={"clip": to}, device_id_type=MESH)
    pl.semaphore_wait(barrier, n - 1 + clips - 1)

    def whole(owner, head, count):
        return pl.ds(pl.multiple_of((owner * heads + head) * HDIM, HDIM), count * HDIM)

    def held(part, head, count):
        return pl.ds((heads * part + head) * HDIM, count * HDIM)

    def piece_of(base, source):
        return pl.ds(pl.multiple_of(base + source * piece, piece), piece)

    def landing(batch, source):
        t, head, count = batch
        buffer, base = ((kk, rows), (vv, rows), (qq, 0))[t // 2]
        return buffer.at[piece_of(base, source), held(t % 2, head, count)]

    def column(batch, owner):
        t, head, count = batch
        return args[t].at[:, whole(owner, head, count)]

    def outgoing(batch, to):
        t, head, count = batch
        return pltpu.make_async_remote_copy(
            src_ref=column(batch, to),
            dst_ref=landing(batch, me),
            send_sem=send.at[head, t, to],
            recv_sem=recv.at[head, t, me],
            device_id={"head": to},
            device_id_type=MESH,
        )

    def incoming(batch, source):
        t, head, count = batch
        return pltpu.make_async_remote_copy(
            src_ref=column(batch, source),
            dst_ref=landing(batch, source),
            send_sem=send.at[head, t, source],
            recv_sem=recv.at[head, t, source],
            device_id={"head": source},
            device_id_type=MESH,
        )

    def stay(batch):
        t, head, count = batch
        return pltpu.make_async_copy(column(batch, me), landing(batch, me), local.at[head, t])

    def forward(batch):
        t, head, count = batch
        buffer, cols = (kk, vv)[t // 2], held(t % 2, head, count)
        return pltpu.make_async_remote_copy(
            src_ref=buffer.at[pl.ds(rows, rows), cols],
            dst_ref=buffer.at[pl.ds(0, rows), cols],
            send_sem=fsend.at[head, t],
            recv_sem=frecv.at[head, t],
            device_id={"clip": after},
            device_id_type=MESH,
        )

    def issue(stage):
        for batch in stage:
            for to, _ in peers:
                outgoing(batch, to).start()
            stay(batch).start()

    def arrive(stage):
        for batch in stage:
            stay(batch).wait()
            for _, source in peers:
                incoming(batch, source).wait_recv()
            if batch[0] < 4:
                forward(batch).start()

    def result_rows(lot, which, owner):
        head, count = lot
        at = pl.ds(pl.multiple_of(owner * piece, piece), piece)
        return oo.at[at, held(which, head, count)]

    def result_home(lot, which, maker):
        return (out, tan)[which].at[:, whole(maker, *lot)]

    def give(lot, which, to):
        return pltpu.make_async_remote_copy(
            src_ref=result_rows(lot, which, to),
            dst_ref=result_home(lot, which, me),
            send_sem=osend.at[lot[0], which, to],
            recv_sem=orecv.at[lot[0], which, me],
            device_id={"head": to},
            device_id_type=MESH,
        )

    def take(lot, which, maker):
        return pltpu.make_async_remote_copy(
            src_ref=result_rows(lot, which, maker),
            dst_ref=result_home(lot, which, maker),
            send_sem=osend.at[lot[0], which, maker],
            recv_sem=orecv.at[lot[0], which, maker],
            device_id={"head": maker},
            device_id_type=MESH,
        )

    def keep(lot, which):
        return pltpu.make_async_copy(
            result_rows(lot, which, me), result_home(lot, which, me), olocal.at[lot[0], which]
        )

    def hand_out(lot, owner):
        @pl.when(owner == me)
        def _():
            for which in range(2):
                keep(lot, which).start()

        @pl.when(owner != me)
        def _():
            for which in range(2):
                give(lot, which, owner).start()

    clip_count = rows // CLIP
    block_rows = min(256, piece)
    per_clip, per_piece = CLIP // block_rows, piece // block_rows
    total_clips = clip_count * clips
    home = me * piece // CLIP

    def block_of(step):
        within = lax.rem(home + 1 + step // per_clip, clip_count)
        return within * per_clip + lax.rem(step, per_clip)

    def is_one(value):
        return jnp.full((16, HDIM), jnp.where(value, 1.0, 0.0), jnp.float32).astype(jnp.bfloat16)

    def attend(head, lot):
        def one_clip(turn, _):
            within = lax.rem(home + 1 + turn, clip_count)
            own = clip_count + within
            clip_id = group * clip_count + within
            gaps = [lax.rem(clip_id - chosen[i, clip_id] + total_clips, total_clips) for i in range(2)]
            near, far = jnp.minimum(*gaps) == 1, jnp.maximum(*gaps) == 2
            flags = [is_one(near), is_one(jnp.logical_not(near)), is_one(far), is_one(jnp.logical_not(far))]
            for place in range(3):
                at = pl.ds(place * CLIP, CLIP)
                for window, rows_held in ((wk, kk), (wv, vv)):
                    for part in range(2):

                        def clip_back(gap):
                            row = pl.multiple_of(lax.max(own - gap, 0) * CLIP, CLIP)
                            return rows_held[pl.ds(row, CLIP), held(part, head, 1)]

                        if place == 0:
                            mixed = clip_back(0)
                        else:
                            first, second = (
                                clip_back(place + i).reshape(CLIP // 16, 16, HDIM) * flags[place * 2 - 2 + i]
                                for i in range(2)
                            )
                            mixed = (first + second).reshape(CLIP, HDIM)
                        window[at, part * HDIM : (part + 1) * HDIM] = mixed

            def one_block(block, _):
                row = within * CLIP + block * block_rows
                at = pl.ds(pl.multiple_of(row, block_rows), block_rows)
                step = turn * per_clip + block
                both = jnp.concatenate([qq[at, held(part, head, 1)] for part in range(2)], axis=1)
                result = attend_rows(both, wk, wv, HDIM**-0.5)
                oo[at, held(0, head, 1)], oo[at, held(1, head, 1)] = result

                if lot is not None:

                    @pl.when(jnp.logical_and(step > 0, lax.rem(step, per_piece) == 0))
                    def _():
                        hand_out(lot, block_of(step - 1) // per_piece)

                return 0

            return lax.fori_loop(0, per_clip, one_block, 0)

        lax.fori_loop(0, clip_count, one_clip, 0)

    tile = 256 if cot.shape[1] % 256 == 0 else HDIM

    def multiply(head):
        flipped[...] = oo[:, held(0, head, 1)].T

        def one_tile(j, _):
            at = pl.ds(pl.multiple_of(j * tile, tile), tile)
            terms[head % 2, :, at] = jnp.dot(
                flipped[...], cot[:, at], preferred_element_type=jnp.float32
            )
            return 0

        lax.fori_loop(0, cot.shape[1] // tile, one_tile, 0)

    def share(owner):
        return pl.ds(pl.multiple_of(owner * wide, HDIM), wide)

    def give_term(head, to, source):
        return pltpu.make_async_remote_copy(
            src_ref=terms.at[head % 2, :, share(to)],
            dst_ref=others.at[head, source],
            send_sem=gsend.at[head, to],
            recv_sem=grecv.at[head, source],
            device_id={"clip": to},
            device_id_type=MESH,
        )

    def reduce_terms(head):
        total = terms[head % 2, :, share(group)]
        for _, source in groups:
            give_term(head, source, source).wait_recv()
            total = total + others[head, source]
        grad[:, head * HDIM : (head + 1) * HDIM] = total.T

    stages, ready = [], []
    for head in range(heads + 1):
        if head < heads:
            stages += [[(t, head, 1), (t + 1, head, 1)] for t in (0, 2)]
            ready += [None, None]
        if head:
            stages.append([(4, head - 1, 1), (5, head - 1, 1)])
            ready.append(head - 1)

    lots = [(i, 1) for i in range(heads)]
    if heads % 2 == 0:
        for i in range(0, heads - 2, 2):
            lots[i], lots[i + 1] = None, (i, 2)

    def compute(head):
        if head == 0:
            choose.wait()
            load.wait()
        for t in range(4):
            forward((t, head, 1)).wait_recv()
        attend(head, lots[head])
        if head >= 2:
            for to, _ in groups:
                give_term(head - 2, to, group).wait_send()
        multiply(head)
        if lots[head] is not None:
            hand_out(lots[head], block_of(rows // block_rows - 1) // per_piece)
        for to, _ in groups:
            give_term(head, to, group).start()
        if head:
            reduce_terms(head - 1)

    load = pltpu.make_async_copy(cotangent, cot, csem.at[0])
    choose = pltpu.make_async_copy(partners, chosen, csem.at[1])
    for stage in stages[:AHEAD]:
        issue(stage)
    choose.start()
    load.start()
    for number, stage in enumerate(stages):
        arrive(stage)
        if number + AHEAD < len(stages):
            issue(stages[number + AHEAD])
        if ready[number] is not None:
            compute(ready[number])
    for stage in stages:
        for batch in stage:
            for to, _ in peers:
                outgoing(batch, to).wait_send()
            if batch[0] < 4:
                forward(batch).wait_send()
    reduce_terms(heads - 1)
    for head in range(max(heads - 2, 0), heads):
        for to, _ in groups:
            give_term(head, to, group).wait_send()
    for lot in lots:
        if lot is not None:
            for which in range(2):
                keep(lot, which).wait()
                for to, maker in peers:
                    give(lot, which, to).wait_send()
                    take(lot, which, maker).wait_recv()


def store_kernel(*refs):
    moves = [pltpu.make_async_copy(refs[i], refs[3 + i], refs[6].at[i]) for i in range(3)]
    for move in moves:
        move.start()
    for move in moves:
        move.wait()


def on_device(
    queries, key_rows, value_rows, query_tangent, key_tangent, value_tangent, partners, cotangent
):
    n, clips = lax.axis_size("head"), lax.axis_size("clip")
    rows, cols = queries.shape[0] * n, queries.shape[1] // n
    heads = cols // HDIM
    width = cotangent.shape[1]
    args = (key_rows, key_tangent, value_rows, value_tangent, query_tangent, queries)
    low, f32 = jnp.bfloat16, jnp.float32
    shapes = [(queries.shape, low), (queries.shape, low), ((width // clips, cols), f32)]
    dma = pltpu.SemaphoreType.DMA
    hbm, vmem = pl.BlockSpec(memory_space=pltpu.HBM), pl.BlockSpec(memory_space=pltpu.VMEM)
    results = pl.pallas_call(
        functools.partial(exchange_kernel, n, clips, heads),
        out_shape=tuple(pltpu.VMEM(*s) for s in shapes),
        in_specs=[hbm] * 8,
        out_specs=[vmem] * 3,
        scratch_shapes=[pltpu.VMEM((2 * rows, 2 * cols), low)] * 2
        + [pltpu.VMEM((rows, 2 * cols), low)] * 2
        + [pltpu.VMEM((3 * CLIP, 2 * HDIM), low)] * 2
        + [
            pltpu.VMEM((rows, width), low),
            pltpu.VMEM((HDIM, rows), low),
            pltpu.VMEM((2, HDIM, width), f32),
            pltpu.VMEM((heads, clips, HDIM, width // clips), f32),
            pltpu.SMEM(partners.shape[::-1], partners.dtype),
        ]
        + [dma((heads, 6, n)), dma((heads, 6, n)), dma((heads, 6)), dma((heads, 4)), dma((heads, 4))]
        + [dma((heads, 2, n)), dma((heads, 2, n)), dma((heads, 2))]
        + [dma((heads, clips)), dma((heads, clips)), dma((2,))],
        compiler_params=pltpu.CompilerParams(
            collective_id=0, has_side_effects=True, vmem_limit_bytes=58 * 1024 * 1024
        ),
        cost_estimate=pl.CostEstimate(
            flops=12 * rows * cols * 3 * CLIP + 2 * rows * cols * width,
            bytes_accessed=16 * rows * cols * 2 + rows * width * 2,
            transcendentals=rows * heads * 3 * CLIP,
        ),
    )(partners.T, *args, cotangent)
    return pl.pallas_call(
        store_kernel,
        out_shape=tuple(jax.ShapeDtypeStruct(*s) for s in shapes),
        in_specs=[vmem] * 3,
        out_specs=[hbm] * 3,
        scratch_shapes=[dma((3,))],
        compiler_params=pltpu.CompilerParams(vmem_limit_bytes=1024 * 1024),
    )(*(pltpu.with_memory_space_constraint(r, pltpu.VMEM) for r in results))


def solution(mesh):
    tokens = P(("clip", "head"), None)
    return jax.shard_map(
        on_device,
        mesh=mesh,
        in_specs=(tokens,) * 6 + (P(), P("clip", None)),
        out_specs=(tokens, tokens, P("clip", "head")),
        check_vma=False,
    )
```

time: 382 us -> 374 us (0.979)
  local copies, waits for them, and re-layouts: 7.93 us -> 0 us
    unnamed x8 -> x0, local copies, waits for them, and re-layouts: 7.93 us -> none
where the time goes in v2:
time: 374 us
  Pallas kernels  373 us (100%)
    pallas_call x1, Pallas kernels, on_device(): pl.pallas_call(functools.partial(exchange_kernel, n, clips, heads), out_s...  370 us

profile of v2, /device:TPU:9, one launch (start us, length us, event | category | flops | bytes accessed | tf_op | source)
XLA Modules:
  0.0 373.8 jit_solution(10768218479052877734)
XLA Ops:
  0.6 370.4 %shard_map.103 = (bf16[256,4096]{1,0:T(8,128)(2,1)S(1)}, bf16[256,4096]{1,0:T(8,128)(2,1)S(1)}, f32[768,512]{1,0:T(8,128)S(1)}) custom-call(s32[2,8]{1,0:T(2,128)} %bitcast.1, bf16[256,4096]{1,0:T(8,128)(2,1)} %refs_0_.1, bf16[256,4096]{1,0:T(8,128)(2,1)} %refs_1_.1, bf16[256,4096]{1,0:T(8,128)(2,1)} %refs_2_.1, bf16[256,4096]{1,0:T(8,128)(2,1)} %refs_3_.1, ...), custom_call_target="tpu_custom_call" | custom-call | flops 45097156608 | bytes 46137344 | tf_op jit(solution)/shard_map/pallas_call | solution.py:349
  371.0 2.6 shard_map.104

commit v3 on v2

--- a/solution.py
+++ b/solution.py
@@ -297,14 +297,22 @@
 
     load = pltpu.make_async_copy(cotangent, cot, csem.at[0])
     choose = pltpu.make_async_copy(partners, chosen, csem.at[1])
+    place = me // 2
+    inner = jnp.logical_and(place > 0, place < n // 2 - 1)
     for stage in stages[:AHEAD]:
         issue(stage)
+
+    @pl.when(inner)
+    def _():
+        for stage in stages[AHEAD:]:
+            issue(stage)
+
     choose.start()
     load.start()
     for number, stage in enumerate(stages):
         arrive(stage)
         if number + AHEAD < len(stages):
-            issue(stages[number + AHEAD])
+            pl.when(jnp.logical_not(inner))(functools.partial(issue, stages[number + AHEAD]))
         if ready[number] is not None:
             compute(ready[number])
     for stage in stages:

time: 374 us -> 374 us (level)
  no operation moved by 1% of the time
where the time goes in v3:
time: 374 us
  Pallas kernels  373 us (100%)
    pallas_call x1, Pallas kernels, on_device(): pl.pallas_call(functools.partial(exchange_kernel, n, clips, heads), out_s...  370 us

profile of v3, /device:TPU:9, one launch (start us, length us, event | category | flops | bytes accessed | tf_op | source)
XLA Modules:
  0.0 373.6 jit_solution(9232709162210777629)
XLA Ops:
  0.6 370.2 %shard_map.103 = (bf16[256,4096]{1,0:T(8,128)(2,1)S(1)}, bf16[256,4096]{1,0:T(8,128)(2,1)S(1)}, f32[768,512]{1,0:T(8,128)S(1)}) custom-call(s32[2,8]{1,0:T(2,128)} %bitcast.1, bf16[256,4096]{1,0:T(8,128)(2,1)} %refs_0_.1, bf16[256,4096]{1,0:T(8,128)(2,1)} %refs_1_.1, bf16[256,4096]{1,0:T(8,128)(2,1)} %refs_2_.1, bf16[256,4096]{1,0:T(8,128)(2,1)} %refs_3_.1, ...), custom_call_target="tpu_custom_call" | custom-call | flops 45097156608 | bytes 46137344 | tf_op jit(solution)/shard_map/pallas_call | solution.py:357
  370.8 2.6 shard_map.104

commit v4 on v2

--- a/solution.py
+++ b/solution.py
@@ -268,7 +268,12 @@
         if head < heads:
             stages += [[(t, head, 1), (t + 1, head, 1)] for t in (0, 2)]
             ready += [None, None]
-        if head:
+        if heads >= 4 and head == 1:
+            stages.append([(4, 0, 2), (5, 0, 2)])
+            ready.append(0)
+        elif heads >= 4 and head == 2:
+            ready[-1] = 1
+        elif head:
             stages.append([(4, head - 1, 1), (5, head - 1, 1)])
             ready.append(head - 1)
 

time: 374 us -> 387 us (1.035)
  Pallas kernels: 373 us -> 385 us
    pallas_call x1, Pallas kernels: 370 us -> 383 us  [on_device(): pl.pallas_call(functools.partial(exchange_kernel, n, clips, heads), out_s...]
where the time goes in v4:
time: 387 us; the launch traced here: 386 us
  Pallas kernels  385 us (99%)
    pallas_call x1, Pallas kernels, on_device(): pl.pallas_call(functools.partial(exchange_kernel, n, clips, heads), out_s...  383 us

profile of v4, /device:TPU:9, one launch (start us, length us, event | category | flops | bytes accessed | tf_op | source)
XLA Modules:
  0.0 386.2 jit_solution(3211878406830592680)
XLA Ops:
  0.6 382.8 %shard_map.103 = (bf16[256,4096]{1,0:T(8,128)(2,1)S(1)}, bf16[256,4096]{1,0:T(8,128)(2,1)S(1)}, f32[768,512]{1,0:T(8,128)S(1)}) custom-call(s32[2,8]{1,0:T(2,128)} %bitcast.1, bf16[256,4096]{1,0:T(8,128)(2,1)} %refs_0_.1, bf16[256,4096]{1,0:T(8,128)(2,1)} %refs_1_.1, bf16[256,4096]{1,0:T(8,128)(2,1)} %refs_2_.1, bf16[256,4096]{1,0:T(8,128)(2,1)} %refs_3_.1, ...), custom_call_target="tpu_custom_call" | custom-call | flops 45097156608 | bytes 46137344 | tf_op jit(solution)/shard_map/pallas_call | solution.py:354
  383.5 2.6 shard_map.104
